TPU v7x, 512 devices: a whole 4x4x16 slice. The times are simulated.
512 devices in a mesh: lat: 64 (over z, x), tm: 8 (over y, core).
Axes of the slice: x: 4, y: 4, z: 16, core: 2. Of those that a mesh axis runs over, the one named last changes fastest.
Arguments:
- fields: bfloat16 [512, 256, 1024], P('lat', 'tm'), may hold values from -16 to 16
Outputs:
- covariance: float32 [256, 256], P('tm')
All inputs are finite; a program needn't handle non-finite values.
Results may differ from a plain program's by a relative error of at most 0.0003.
Values may be sent and summed in bfloat16 or wider, within the bound.
A program may use at most 64 MiB of HBM per device.

v0:
```python
import functools
import math

import jax
import jax.numpy as jnp
from jax import lax
from jax.sharding import Mesh
from jax.sharding import PartitionSpec as P

TRUNC = 341
MSLOT = 384
DSLOT = 384
LAT = ("lat_0", "lat_1")


def split_up(value, dim, length):
    dims = value.shape
    blocks = value.reshape(*dims[:dim], length, dims[dim] // length, *dims[dim + 1 :])
    return jnp.moveaxis(blocks, dim, 0)


def sum_at_owner(value, axis, dim):
    length = lax.axis_size(axis)
    blocks = lax.all_to_all(split_up(value, dim, length), axis, 0, 0, tiled=True)
    return jnp.sum(blocks, axis=0)


def one_axis_at_a_time(value, axes):
    return functools.reduce(lax.psum, axes, value)


def from_everyone(value, axis):
    length = lax.axis_size(axis)
    return lax.all_to_all(
        jnp.broadcast_to(value[None], (length, *value.shape)), axis, 0, 0, tiled=True
    )


def of_everyone(value, axis):
    return from_everyone(value, axis).sum(axis=0)


def start_value(order, sine_lat):
    log_start = 0.5 * (
        math.log(0.5)
        + lax.lgamma(order + 1.5)
        - (0.5 * math.log(math.pi) - math.log(2.0))
        - lax.lgamma(order + 1.0)
    ) + order * jnp.log(sine_lat)
    taper = jnp.clip((log_start + 70.0) / 10.0, 0.0, 1.0)
    return jnp.exp(jnp.maximum(log_start, -80.0)) * taper


def step_factors(order, degree):
    top = jnp.sqrt((4.0 * degree * degree - 1.0) / (degree * degree - order * order))
    below = degree - 1.0
    back = jnp.sqrt(
        jnp.maximum(below * below - order * order, 0.0) / jnp.abs(4.0 * below * below - 1.0)
    )
    return (top, top * back)


def legendre_blocks(orders, cosine_lat, sine_lat):
    order_total = orders.shape[0]
    lat_total = cosine_lat.shape[0]
    block_total = 16
    block_length = DSLOT // block_total
    order_grid = orders[:, None, None]
    cosine_grid = cosine_lat[None, :, None]
    block_base = (jnp.arange(block_total) * block_length).astype(jnp.float32)[None, None, :]
    unit = jnp.ones((order_total, lat_total, block_total), jnp.float32)
    empty = jnp.zeros_like(unit)

    def compose(position, matrices):
        upper_left, upper_right, lower_left, lower_right = matrices
        top, mixed = step_factors(
            order_grid, order_grid + block_base + position.astype(jnp.float32)
        )
        diagonal_term = top * cosine_grid
        return (
            diagonal_term * upper_left - mixed * lower_left,
            diagonal_term * upper_right - mixed * lower_right,
            upper_left,
            upper_right,
        )

    upper_left, upper_right, lower_left, lower_right = lax.fori_loop(
        1, block_length + 1, compose, (unit, empty, empty, unit)
    )
    current = start_value(orders[:, None], sine_lat[None, :])
    previous = jnp.zeros_like(current)
    current_list = []
    previous_list = []
    for block in range(block_total):
        current_list.append(current)
        previous_list.append(previous)
        current, previous = (
            upper_left[:, :, block] * current + upper_right[:, :, block] * previous,
            lower_left[:, :, block] * current + lower_right[:, :, block] * previous,
        )
    current = jnp.stack(current_list, axis=-1)
    previous = jnp.stack(previous_list, axis=-1)
    outputs = []
    for position in range(1, block_length + 1):
        outputs.append(current)
        top, mixed = step_factors(order_grid, order_grid + block_base + float(position))
        current, previous = (top * cosine_grid * current - mixed * previous, current)
    values = jnp.stack(outputs, axis=-1)
    return values.reshape(order_total, lat_total, DSLOT)


def weighted_basis(orders, cosine_lat, sine_lat, weight):
    values = legendre_blocks(orders, cosine_lat, sine_lat)
    offsets = jnp.arange(DSLOT).astype(jnp.float32)
    keep = (orders[:, None] + offsets[None, :] <= TRUNC).astype(jnp.float32)
    factor = jnp.where(orders > 0, math.sqrt(2.0), 1.0)
    table = values * keep[:, None, :] * weight[None, :, None] * factor[:, None, None]
    return table.astype(jnp.bfloat16)


def local(fields):
    row_count, month_count, lon_count = fields.shape
    lat_devices = lax.axis_size(LAT)
    slots_dev = MSLOT // lat_devices
    lat_index = lax.axis_index(LAT)
    column = jnp.arange(2 * MSLOT)
    group = column // (2 * slots_dev)
    inner = column % (2 * slots_dev) // 2
    part_index = column % 2
    own_inner = jnp.arange(slots_dev)
    wave_order = group * slots_dev + inner
    own_order = lat_index * slots_dev + own_inner
    longitude = jnp.arange(lon_count)
    phase = (
        2.0
        * math.pi
        * (wave_order[:, None] * longitude[None, :] % lon_count).astype(jnp.float32)
        / lon_count
    )
    active = (wave_order <= TRUNC).astype(jnp.float32)[:, None]
    transform = (
        jnp.where(part_index[:, None] == 0, jnp.cos(phase), -jnp.sin(phase))
        * active
        / math.sqrt(lon_count)
    )
    transform = transform.astype(jnp.bfloat16)
    flat_fields = fields.reshape(row_count * month_count, lon_count)
    fourier = lax.dot_general(
        transform, flat_fields, (((1,), (1,)), ((), ())), preferred_element_type=jnp.float32
    )
    fourier = fourier.astype(jnp.bfloat16).reshape(2 * MSLOT, row_count, month_count)
    moved = lax.all_to_all(fourier, LAT, split_axis=0, concat_axis=1, tiled=True)
    lat_count = moved.shape[1]
    theta = math.pi * (jnp.arange(lat_count).astype(jnp.float32) + 0.5) / lat_count
    cosine_lat = jnp.cos(theta)
    sine_lat = jnp.sin(theta)
    weight = math.pi * sine_lat / lat_count
    basis = weighted_basis(own_order.astype(jnp.float32), cosine_lat, sine_lat, weight)
    moved_data = moved.reshape(slots_dev, 2, lat_count, month_count)
    coefficients = jnp.einsum(
        "srjt,sjd->tsrd", moved_data, basis, preferred_element_type=jnp.float32
    )
    coefficients = coefficients.astype(jnp.bfloat16).reshape(month_count, -1)
    tm_devices = lax.axis_size("tm")
    total_months = month_count * tm_devices
    columns = lax.all_to_all(coefficients, "tm", split_axis=1, concat_axis=0, tiled=True)
    partial_gram = sum_at_owner(
        lax.dot_general(
            columns, columns, (((1,), (1,)), ((), ())), preferred_element_type=jnp.float32
        ),
        "tm",
        0,
    )
    gram = one_axis_at_a_time(partial_gram, LAT)
    own_block = lax.dynamic_slice_in_dim(gram, lax.axis_index("tm") * month_count, month_count, 1)
    trace_total = of_everyone(jnp.sum(jnp.diagonal(own_block)), "tm")
    return total_months * gram / (trace_total + 1e-06)


def solution(mesh):
    torus = Mesh(mesh.devices.reshape(16, 4, mesh.shape["tm"]), ("lat_0", "lat_1", "tm"))
    placed = (P(LAT, "tm", None),)
    return jax.shard_map(
        local, mesh=torus, in_specs=placed, out_specs=P("tm", None), check_vma=False
    )
```

profile of v0, /device:TPU:1, one launch (start us, length us, event | category | flops | bytes accessed | tf_op | source)
XLA Modules:
  0.0 193.9 jit_solution(4032338492289574564)
XLA Ops:
  0.0 1.0 copy-done
  1.0 14.9 %fusion.36 = bf16[768,256]{0,1:T(8,128)(2,1)S(1)} fusion(bf16[256,1024]{1,0:T(8,128)(2,1)S(1)} %bitcast.85, f32[768]{0:T(1024)S(1)} %get-tuple-element.432, s32[768]{0:T(1024)S(1)} %fusion.118, pred[768]{0:T(1024)(128)(4,1)S(1)} %get-tuple-element.431), kind=kOutput, calls=%fused_computation.50 | convolution fusion | flops 417792000 | bytes 924416 | tf_op jit(solution)/shard_map/dot_general | solution.py:148
  15.9 1.1 copy.122
  17.0 1.9 reshape.8830
  18.9 19.3 %all-to-all-start = ((bf16[64,2,1536]{2,1,0:T(2,128)(2,1)}), bf16[64,2,1536]{2,1,0:T(2,128)(2,1)S(1)}, u32[]{:S(2)}, u32[]{:S(2)}) async-start(bf16[64,2,1536]{2,1,0:T(2,128)(2,1)} %reshape.8830), calls=%async_computation | async-start | bytes 786432 | tf_op jit(solution)/shard_map/all_to_all | solution.py:152
  38.4 10.6 %while.25 = (s32[]{:T(128)}, f32[6,512,16]{1,2,0:T(8,128)S(1)}, f32[6,512,16]{1,2,0:T(8,128)S(1)}, f32[6,512,16]{1,2,0:T(8,128)S(1)}, f32[6,512,16]{1,2,0:T(8,128)S(1)}, /*index=5*/s32[]{:T(128)}, s32[]{:T(128)}, s32[]{:T(128)}) while((s32[]{:T(128)}, f32[6,512,16]{1,2,0:T(8,128)S(1)}, ...), condition=%wide.region_1.2_spmd.clone.clone.clone, body=%wide.region_0.1_spmd.clone.clone.clone.sunk | while | flops 445698 | bytes 1578843 | solution.py:87
  49.1 0.7 add_bitcast_fusion
  50.2 0.7 bitcast_dynamic-update-slice_fusion
  51.7 0.8 constant_dynamic-update-slice_fusion.19
  52.5 0.8 constant_dynamic-update-slice_fusion.18
  53.3 0.8 constant_dynamic-update-slice_fusion.17
  54.1 0.9 constant_dynamic-update-slice_fusion.16
  55.0 0.8 constant_dynamic-update-slice_fusion.15
  55.8 0.8 constant_dynamic-update-slice_fusion.14
  56.6 0.8 constant_dynamic-update-slice_fusion.13
  57.5 0.9 constant_dynamic-update-slice_fusion.12
  58.3 0.8 constant_dynamic-update-slice_fusion.11
  59.1 0.8 constant_dynamic-update-slice_fusion.10
  60.0 0.9 constant_dynamic-update-slice_fusion.9
  60.8 0.8 constant_dynamic-update-slice_fusion.8
  61.7 0.8 constant_dynamic-update-slice_fusion.7
  62.5 0.8 constant_dynamic-update-slice_fusion.6
  63.3 0.9 constant_dynamic-update-slice_fusion.5
  64.2 0.9 constant_dynamic-update-slice_fusion.4
  65.0 0.8 constant_dynamic-update-slice_fusion.3
  65.8 0.8 constant_dynamic-update-slice_fusion.2
  66.6 0.8 constant_dynamic-update-slice_fusion.1
  67.5 0.8 constant_dynamic-update-slice_fusion
  68.2 0.8 fusion.40
  69.1 0.8 fusion.39
  69.9 0.9 subtract_dynamic-update-slice_fusion
  70.8 5.0 %copy.121 = f32[6,512,16,24]{1,3,2,0:T(8,128)S(1)} copy(f32[6,512,16,24]{1,2,3,0:T(8,128)} %subtract_dynamic-update-slice_fusion) | data formatting | bytes 9437184 | tf_op jit(solution)/shard_map/stack | solution.py:108
  75.9 0.6 fusion.20
  76.6 2.0 %reshape.8831 = bf16[768,8,32]{2,1,0:T(8,128)(2,1)} reshape(bf16[64,2,1536]{2,1,0:T(2,128)(2,1)S(1)} %all-to-all-done) | data formatting | bytes 786432
  78.6 2.9 %copy.123 = bf16[12,64,8,32]{3,2,1,0:T(8,128)(2,1)} copy(bf16[12,64,8,32]{3,2,0,1:T(8,128)(2,1)} %bitcast.86) | data formatting | bytes 786432 | tf_op jit(solution)/shard_map/all_to_all | solution.py:152
  81.5 1.6 copy.125
  83.1 0.8 fusion.355
  84.7 12.7 %all_to_all.45 = bf16[32,8,576]{2,0,1:T(8,128)(2,1)S(1)} all-to-all(bf16[32,8,576]{2,0,1:T(8,128)(2,1)S(1)} %copy.127), channel_id=1, replica_groups=mesh['lat_0'=16,'lat_1'=4,'tm'=8] {'tm'}, dimensions={1} | all-to-all | bytes 589824 | tf_op jit(solution)/shard_map/all_to_all | solution.py:166
  97.4 1.0 fusion.37
  98.4 4.1 %all-to-all-start.2 = ((f32[8,32,256]{2,1,0:T(8,128)}), f32[8,32,256]{2,1,0:T(8,128)S(1)}, u32[]{:S(2)}, u32[]{:S(2)}) async-start(f32[8,32,256]{2,1,0:T(8,128)} %fusion.37), calls=%async_computation.2 | async-start | bytes 524288 | tf_op jit(solution)/shard_map/all_to_all | solution.py:24
  102.4 6.5 %all-to-all-done.2 = f32[8,32,256]{2,1,0:T(8,128)S(1)} async-done(((f32[8,32,256]{2,1,0:T(8,128)}), f32[8,32,256]{2,1,0:T(8,128)S(1)}, u32[]{:S(2)}, u32[]{:S(2)}) %all-to-all-start.2) | async-done | bytes 262176 | tf_op jit(solution)/shard_map/all_to_all | solution.py:24
  109.0 42.4 %psum.14 = f32[32,256]{1,0:T(8,128)S(1)} all-reduce(f32[32,256]{1,0:T(8,128)S(1)} %reduce_sum.27), channel_id=1, replica_groups=mesh['lat_0'=16,'lat_1'=4,'tm'=8] {'lat_0'}, use_global_device_ids=true, to_apply=%region_3.4 | all-reduce | flops 8192 | bytes 65536 | tf_op jit(solution)/shard_map/psum | solution.py:29
  151.3 13.2 %psum.15 = f32[32,256]{1,0:T(8,128)S(1)} all-reduce(f32[32,256]{1,0:T(8,128)S(1)} %psum.14), channel_id=1, replica_groups=mesh['lat_0'=16,'lat_1'=4,'tm'=8] {'lat_1'}, use_global_device_ids=true, to_apply=%region_4.5 | all-reduce | flops 8192 | bytes 65536 | tf_op jit(solution)/shard_map/psum | solution.py:29
  164.7 0.7 gather_fusion
  166.0 0.6 broadcast_in_dim.26
  166.6 25.4 %all_to_all.46 = f32[8,1,1]{2,1,0:T(1,128)S(1)} all-to-all(f32[8,1,1]{2,1,0:T(1,128)S(1)} %broadcast_in_dim.26), channel_id=1, replica_groups=mesh['lat_0'=16,'lat_1'=4,'tm'=8] {'tm'}, dimensions={0} | all-to-all | bytes 64 | tf_op jit(solution)/shard_map/all_to_all | solution.py:34
  192.0 0.6 reduce_sum.29
  193.3 0.6 multiply_divide_fusion
  (176 shorter events, 12.4 us)
Async XLA Ops:
  0.0 1.0 copy-start
  18.9 57.7 %all-to-all-start = ((bf16[64,2,1536]{2,1,0:T(2,128)(2,1)}), bf16[64,2,1536]{2,1,0:T(2,128)(2,1)S(1)}, u32[]{:S(2)}, u32[]{:S(2)}) async-start(bf16[64,2,1536]{2,1,0:T(2,128)(2,1)} %reshape.8830), calls=%async_computation | async-start | bytes 786432 | tf_op jit(solution)/shard_map/all_to_all | solution.py:152
  98.4 10.6 %all-to-all-start.2 = ((f32[8,32,256]{2,1,0:T(8,128)}), f32[8,32,256]{2,1,0:T(8,128)S(1)}, u32[]{:S(2)}, u32[]{:S(2)}) async-start(f32[8,32,256]{2,1,0:T(8,128)} %fusion.37), calls=%async_computation.2 | async-start | bytes 524288 | tf_op jit(solution)/shard_map/all_to_all | solution.py:24
where the time goes:
time: 194 us
  blocking collectives  93.7 us (48%)
  other arithmetic  32.3 us (17%)
  starting transfers between devices  23.3 us (12%)
  local copies, waits for them, and re-layouts  19.3 us (10%)
  matrix products  16.7 us (9%)
  waiting for transfers between devices  6.49 us (3%)
    psum x2, blocking collectives, one_axis_at_a_time(): return functools.reduce(lax.psum, axes, value)  55.6 us
    all_to_all x1, blocking collectives, from_everyone(): lax.all_to_all(jnp.broadcast_to(value[None], (length, *value.shape)), axi...  25.4 us
    all_to_all x1, starting transfers between devices, local(): lax.all_to_all(fourier, LAT, split_axis=0, concat_axis=1, tiled=True)  19.3 us
    unnamed x24, other arithmetic  18.2 us
    dot_general x1, matrix products, local(): lax.dot_general(transform, flat_fields, (((1,), (1,)), ((), ())), preferr...  14.9 us
    all_to_all x1, blocking collectives, local(): lax.all_to_all(coefficients, 'tm', split_axis=1, concat_axis=0, tiled=True)  12.7 us
    all_to_all x1, waiting for transfers between devices, sum_at_owner(): lax.all_to_all(split_up(value, dim, length), axis, 0, 0, tiled=True)  6.49 us
    unnamed x5, local copies, waits for them, and re-layouts  5.59 us
  transfers between devices with their start and end apart: 2, of which 1 were waited for; matrix products, arithmetic and copies ran while one was open for 19% of the time, Pallas kernels for 0%

commit v1 on v0

v1 whole, which is shorter than its diff:
```python
import functools
import math

import jax
import jax.numpy as jnp
from jax import lax
from jax.experimental import pallas as pl
from jax.experimental.pallas import tpu as pltpu
from jax.sharding import PartitionSpec as P

TRUNC = 341
NLON = 1024
NLAT = 512
MONTHS = 256
OWNERS = 57
SLOTS = 6
PAIRS = 3
DEPTH = (384, 256, 128)
FIRST_ROW = (0, 384, 640)
ROWS = 768
PITCH = 60
NX = 4
NZ = 16
LATS = 64
TMS = 8
BLOCK = 8
LOCAL = 32
MESH = pl.DeviceIdType.MESH
F32 = jnp.float32
BF16 = jnp.bfloat16
SINE = tuple(
    (-1.0) ** k * (2.0 * math.pi) ** (2 * k + 1) / math.factorial(2 * k + 1) for k in range(7)
)


def sine_of_turns(u):
    square = u * u
    total = jnp.full_like(u, SINE[6])
    for k in range(5, -1, -1):
        total = total * square + SINE[k]
    return total * u


def transform_rows(step):
    pair = step // 15
    sub = lax.broadcasted_iota(jnp.int32, (16, NLON), 0)
    lon = lax.broadcasted_iota(jnp.int32, (16, NLON), 1)
    wave = (step % 15) * 4 + (sub >> 2) + OWNERS * (2 * pair + ((sub >> 1) & 1))
    phase = (wave * lon + 256 * (sub & 1)) & 1023
    away = jnp.abs(((phase + 512) & 1023) - 512)
    return sine_of_turns((256 - away).astype(F32) * (1.0 / NLON)) * (1.0 / math.sqrt(NLON))


def roll(value, shift, axis):
    return pltpu.roll(value, shift % value.shape[axis], axis)


def swap_bit(value, bit):
    rows = value.shape[0]
    sub = (lax.broadcasted_iota(jnp.int32, (rows, 128), 0) >> bit) & 1
    group = (lax.broadcasted_iota(jnp.int32, (rows, 128), 1) >> (5 + bit)) & 1
    step = 1 << bit
    from_below = roll(roll(value, 32 * step, 1), -step, 0)
    from_above = roll(roll(value, -32 * step, 1), step, 0)
    return jnp.where(sub == group, value, jnp.where(sub == 0, from_below, from_above))


def rows_by_latitude(spectrum):
    rows = spectrum.shape[0]
    low, high = spectrum[:, :128], spectrum[:, 128:]
    upper = ((lax.broadcasted_iota(jnp.int32, (rows, 128), 0) >> 2) & 1) == 0
    even = jnp.where(upper, low, roll(high, 4, 0))
    odd = jnp.where(upper, roll(low, -4, 0), high)
    return [swap_bit(swap_bit(part, 0), 1) for part in (even, odd)]


def start_value(order, sine_lat):
    ratio = jnp.ones_like(order)
    for step in range(1, 9):
        ratio = ratio * ((order + step) / (order + (step + 0.5)))
    far = order + 9.0
    inverse = 1.0 / far
    square = inverse * inverse
    series = inverse * (-1.0 / 8.0 + square * (1.0 / 192.0 - square * (1.0 / 640.0)))
    log_ratio = 0.5 * jnp.log(far) + series + jnp.log(ratio)
    constant = math.log(0.5) - (0.5 * math.log(math.pi) - math.log(2.0))
    log_start = 0.5 * (constant + log_ratio) + order * jnp.log(sine_lat)
    taper = jnp.clip((log_start + 70.0) / 10.0, 0.0, 1.0)
    return jnp.exp(jnp.maximum(log_start, -80.0)) * taper


def step_factors(order, degree):
    top = jnp.sqrt((4.0 * degree * degree - 1.0) / (degree * degree - order * order))
    below = degree - 1.0
    back = jnp.sqrt(
        jnp.maximum(below * below - order * order, 0.0) / jnp.abs(4.0 * below * below - 1.0)
    )
    return top, top * back


def legendre(owner, lane_offset):
    sub = lax.broadcasted_iota(jnp.int32, (8, 128), 0)
    order = (jnp.minimum(sub, SLOTS - 1) * OWNERS + owner).astype(F32)
    place = (lax.broadcasted_iota(jnp.int32, (8, 128), 1) + lane_offset).astype(F32) + 0.5
    turn = place * (0.5 / NLAT)
    folded = jnp.minimum(turn, 0.5 - turn)
    half = sine_of_turns(0.5 * folded)
    cosine = jnp.where(folded < 0.125, 1.0 - 2.0 * half * half, sine_of_turns(0.25 - folded))
    cosine_lat = jnp.where(turn < 0.25, cosine, -cosine)
    return order, cosine_lat, sine_of_turns(folded)


def lat_weight(width):
    turn = (lax.broadcasted_iota(jnp.int32, (1, width), 1).astype(F32) + 0.5) * (0.5 / NLAT)
    return sine_of_turns(jnp.minimum(turn, 0.5 - turn)) * (math.pi / NLAT)


def regroup(pieces):
    group = lax.broadcasted_iota(jnp.int32, (96, 128), 1) >> 5
    blocks = []
    for g in range(4):
        halves = []
        for half in range(2):
            total = None
            for a in range(4):
                moved = pieces[4 * half + a]
                if a != g:
                    moved = roll(moved, 32 * (a - g), 1)
                total = moved if total is None else jnp.where(group == a, moved, total)
            halves.append(total)
        blocks.append(jnp.concatenate(halves, axis=1))
    return jnp.concatenate(blocks, axis=0)


def owner_of(lat):
    return jnp.where(lat < 28, lat, lat - 7)


def is_owner(lat):
    return jnp.logical_or(lat < 28, lat >= 35)


def kernel(
    fields_hbm,
    out_ref,
    fields,
    transform,
    send,
    got,
    values,
    basis,
    coef,
    share,
    gram,
    slabs,
    planes,
    local_sem,
    send_sem,
    row_sem,
    month_sem,
    slab_sem,
    plane_sem,
    last_sem,
):
    lat = lax.axis_index("lat")
    tm = lax.axis_index("tm")
    z = lat // NX
    x = lat % NX
    load = pltpu.make_async_copy(fields_hbm, fields, local_sem)
    load.start()
    got[...] = jnp.zeros_like(got)

    barrier = pltpu.get_barrier_semaphore()

    def greet_lat(step, carry):
        peer = lax.rem(lat + step, LATS)
        pl.semaphore_signal(barrier, inc=1, device_id={"lat": peer}, device_id_type=MESH)
        return carry

    lax.fori_loop(1, LATS, greet_lat, 0)

    def greet_plane(step, carry):
        peer_tm = lax.rem(tm + 1 + step // NX, TMS)
        peer = z * NX + step % NX
        pl.semaphore_signal(
            barrier, inc=1, device_id={"lat": peer, "tm": peer_tm}, device_id_type=MESH
        )
        return carry

    lax.fori_loop(0, NX * (TMS - 1), greet_plane, 0)

    def fill(step, carry):
        start = pl.multiple_of(step * 16, 16)
        transform[pl.ds(start, 16), :] = transform_rows(step).astype(BF16)
        return carry

    lax.fori_loop(0, 45, fill, 0)
    load.wait()
    flat = fields[...].reshape(BLOCK * LOCAL, NLON)
    for pair in range(PAIRS):
        spectrum = lax.dot_general(
            transform[pair * 240 : (pair + 1) * 240, :],
            flat,
            (((1,), (1,)), ((), ())),
            preferred_element_type=F32,
        )
        for odd, part in enumerate(rows_by_latitude(spectrum)):
            send[:, odd, :, pair * 128 : (pair + 1) * 128] = part.reshape(
                PITCH // 2, BLOCK, 128
            ).astype(BF16)

    own = jnp.where(is_owner(lat), owner_of(lat), 400)

    @pl.when(is_owner(lat))
    def _():
        got[lat] = send[own // 2, own % 2]

    pl.semaphore_wait(barrier, LATS - 1 + NX * (TMS - 1))

    def row_copy(source, target, width):
        peer = owner_of(target)
        return pltpu.make_async_remote_copy(
            src_ref=send.at[peer // 2, peer % 2, :, pl.ds(0, width)],
            dst_ref=got.at[source, :, pl.ds(0, width)],
            send_sem=send_sem.at[0],
            recv_sem=row_sem.at[source],
            device_id={"lat": target},
            device_id_type=MESH,
        )

    near = jnp.minimum(lat, LATS - 1 - lat)
    kinds = (
        (near < 11, 128),
        (jnp.logical_and(near >= 11, near < 16), 256),
        (near >= 16, 384),
    )
    for applies, width in kinds:

        @pl.when(applies)
        def _(width=width):
            def send_both(step, carry):
                away = 32 - step

                for target in (lax.rem(lat + away, LATS), lax.rem(lat + LATS - away, LATS)):

                    @pl.when(is_owner(target))
                    def _(target=target):
                        row_copy(lat, target, width).start()

                return carry

            target = lax.rem(lat + 32, LATS)

            @pl.when(is_owner(target))
            def _():
                row_copy(lat, target, width).start()

            lax.fori_loop(1, 32, send_both, 0)

    order, _, _ = legendre(own, 0)
    cosines = []
    state = []
    for block in range(4):
        _, cosine_lat, sine_lat = legendre(own, 128 * block)
        cosines.append(cosine_lat)
        first = start_value(order, sine_lat)
        values[block, 0:8, :] = first
        state.append(first)
        state.append(jnp.zeros_like(first))

    def advance(trip, carry):
        carry = list(carry)
        for inner in range(1, 9):
            offset = trip * 8 + inner
            top, mixed = step_factors(order, order + offset.astype(F32))
            row = pl.multiple_of(offset * 8, 8)
            for block in range(4):
                current, previous = carry[2 * block], carry[2 * block + 1]
                following = top * cosines[block] * current - mixed * previous
                values[block, pl.ds(row, 8), :] = following
                carry[2 * block], carry[2 * block + 1] = following, current
        return tuple(carry)

    lax.fori_loop(0, 48, advance, tuple(state))
    weight = lat_weight(NLAT)
    for slot in range(SLOTS):
        depth = DEPTH[slot // 2]
        wave = own + OWNERS * slot
        factor = jnp.where(wave > 0, math.sqrt(2.0), 1.0).astype(F32)
        offset = lax.broadcasted_iota(jnp.int32, (depth, 128), 0)
        for block in range(4):
            lanes = slice(128 * block, 128 * (block + 1))
            table = values[block, pl.ds(slot, depth, stride=8), :]
            table = jnp.where(offset + wave <= TRUNC, table * (weight[:, lanes] * factor), 0.0)
            basis[slot, 0:depth, lanes] = table.astype(BF16)

    @pl.when(is_owner(lat))
    def _():
        for first, last, width in (
            (0, 11, 128),
            (11, 16, 256),
            (16, 48, 384),
            (48, 53, 256),
            (53, 64, 128),
        ):

            def receive(source, carry, width=width):
                @pl.when(source != lat)
                def _():
                    row_copy(source, lat, width).wait_recv()

                return carry

            lax.fori_loop(first, last, receive, 0)

    for pair in range(PAIRS):
        depth = DEPTH[pair]
        lo, hi = (16, 48) if pair == 2 else (0, 64)
        data = got[lo:hi, :, pair * 128 : (pair + 1) * 128].astype(F32)
        data = data.reshape((hi - lo) * BLOCK, 128).astype(BF16)
        both = [
            lax.dot_general(
                basis[2 * pair + side, 0:depth, lo * BLOCK : hi * BLOCK],
                data,
                (((1,), (0,)), ((), ())),
                preferred_element_type=F32,
            )
            for side in range(2)
        ]
        lane = lax.broadcasted_iota(jnp.int32, (depth, 128), 1)
        coef[FIRST_ROW[pair] : FIRST_ROW[pair] + depth, :] = jnp.where(
            lane < 64, both[0], both[1]
        ).astype(BF16)

    def month_copy(source, target):
        return pltpu.make_async_remote_copy(
            src_ref=coef.at[pl.ds(pl.multiple_of(target * 96, 96), 96), :],
            dst_ref=share.at[source],
            send_sem=send_sem.at[1],
            recv_sem=month_sem.at[source],
            device_id={"tm": target},
            device_id_type=MESH,
        )

    for step in range(1, TMS):
        month_copy(tm, lax.rem(tm + step, TMS)).start()
    share[tm] = coef[pl.ds(pl.multiple_of(tm * 96, 96), 96), :]
    for step in range(1, TMS):
        month_copy(lax.rem(tm + step, TMS), tm).wait_recv()
    columns = regroup([share[source].astype(F32) for source in range(TMS)]).astype(BF16)
    terms = lax.dot_general(
        columns, columns, (((0,), (0,)), ((), ())), preferred_element_type=F32
    )
    row = lax.broadcasted_iota(jnp.int32, (MONTHS, MONTHS), 0)
    col = lax.broadcasted_iota(jnp.int32, (MONTHS, MONTHS), 1)
    diagonal = jnp.where(row == col, terms, 0.0)
    trace = jnp.sum(jnp.sum(diagonal, axis=0, keepdims=True), axis=1, keepdims=True)
    spare = jnp.logical_and((row & 7) == 1, col == row - 1)
    gram[...] = jnp.where(spare, trace, terms).reshape(32, 8, MONTHS)

    def slab_copy(source, target_x, target_tm):
        return pltpu.make_async_remote_copy(
            src_ref=gram.at[target_tm * NX + target_x],
            dst_ref=slabs.at[source],
            send_sem=send_sem.at[2],
            recv_sem=slab_sem.at[source],
            device_id={"lat": z * NX + target_x, "tm": target_tm},
            device_id_type=MESH,
        )

    me = tm * NX + x

    def send_slab(step, carry):
        target = lax.rem(me + step, 32)
        slab_copy(me, target % NX, target // NX).start()
        return carry

    lax.fori_loop(1, 32, send_slab, 0)
    slabs[me] = gram[me]

    def receive_slab(step, carry):
        slab_copy(lax.rem(me + step, 32), x, tm).wait_recv()
        return carry

    lax.fori_loop(1, 32, receive_slab, 0)
    planes[z] = jnp.sum(slabs[...], axis=0)

    def plane_copy(source, target):
        return pltpu.make_async_remote_copy(
            src_ref=planes.at[z],
            dst_ref=planes.at[source],
            send_sem=send_sem.at[3],
            recv_sem=plane_sem.at[source],
            device_id={"lat": target * NX + x},
            device_id_type=MESH,
        )

    for away in (8, 7, 9, 6, 10, 5, 11, 4, 12, 3, 13, 2, 14, 1, 15):
        plane_copy(z, lax.rem(z + away, NZ)).start()
    for away in range(1, NZ):
        plane_copy(lax.rem(z + away, NZ), z).wait_recv()
    slab = jnp.sum(planes[...], axis=0)
    row = lax.broadcasted_iota(jnp.int32, (BLOCK, MONTHS), 0)
    col = lax.broadcasted_iota(jnp.int32, (BLOCK, MONTHS), 1) - 8 * me
    spare = jnp.logical_and(row == 1, col == 0)
    twin = jnp.logical_and(row == 0, col == 1)

    def pick(mask):
        chosen = jnp.sum(jnp.where(mask, slab, 0.0), axis=0, keepdims=True)
        return jnp.sum(chosen, axis=1, keepdims=True)

    total = pick(spare)
    out_ref[x] = jnp.where(spare, pick(twin), slab) * (MONTHS / (total + 1e-06))

    def last_copy(source, target):
        return pltpu.make_async_remote_copy(
            src_ref=out_ref.at[source],
            dst_ref=out_ref.at[source],
            send_sem=send_sem.at[4],
            recv_sem=last_sem.at[source],
            device_id={"lat": z * NX + target},
            device_id_type=MESH,
        )

    for away in (2, 1, 3):
        last_copy(x, lax.rem(x + away, NX)).start()
    for away in range(1, NX):
        last_copy(lax.rem(x + away, NX), x).wait_recv()

    for applies, width in kinds:

        @pl.when(applies)
        def _(width=width):
            def sent(step, carry):
                target = lax.rem(lat + step, LATS)

                @pl.when(is_owner(target))
                def _():
                    row_copy(lat, target, width).wait_send()

                return carry

            lax.fori_loop(1, LATS, sent, 0)

    for step in range(1, TMS):
        month_copy(tm, lax.rem(tm + step, TMS)).wait_send()

    def slab_sent(step, carry):
        target = lax.rem(me + step, 32)
        slab_copy(me, target % NX, target // NX).wait_send()
        return carry

    lax.fori_loop(1, 32, slab_sent, 0)
    for away in range(1, NZ):
        plane_copy(z, lax.rem(z + away, NZ)).wait_send()
    for away in range(1, NX):
        last_copy(x, lax.rem(x + away, NX)).wait_send()


def local(fields):
    call = pl.pallas_call(
        kernel,
        out_shape=jax.ShapeDtypeStruct((NX, BLOCK, MONTHS), F32),
        in_specs=[pl.BlockSpec(memory_space=pl.ANY)],
        out_specs=pl.BlockSpec(memory_space=pltpu.VMEM),
        scratch_shapes=[
            pltpu.VMEM((BLOCK, LOCAL, NLON), BF16),
            pltpu.VMEM((PAIRS * 240, NLON), BF16),
            pltpu.VMEM((PITCH // 2, 2, BLOCK, 384), BF16),
            pltpu.VMEM((LATS, BLOCK, 384), BF16),
            pltpu.VMEM((4, 385 * 8, 128), F32),
            pltpu.VMEM((SLOTS, 384, NLAT), BF16),
            pltpu.VMEM((ROWS, 128), BF16),
            pltpu.VMEM((TMS, 96, 128), BF16),
            pltpu.VMEM((32, BLOCK, MONTHS), F32),
            pltpu.VMEM((32, BLOCK, MONTHS), F32),
            pltpu.VMEM((NZ, BLOCK, MONTHS), F32),
            pltpu.SemaphoreType.DMA,
            pltpu.SemaphoreType.DMA((5,)),
            pltpu.SemaphoreType.DMA((LATS,)),
            pltpu.SemaphoreType.DMA((TMS,)),
            pltpu.SemaphoreType.DMA((32,)),
            pltpu.SemaphoreType.DMA((NZ,)),
            pltpu.SemaphoreType.DMA((NX,)),
        ],
        compiler_params=pltpu.CompilerParams(
            collective_id=0, has_side_effects=True, vmem_limit_bytes=48 * 1024 * 1024
        ),
    )
    return call(fields).reshape(LOCAL, MONTHS)


def solution(mesh):
    return jax.shard_map(
        local,
        mesh=mesh,
        in_specs=(P("lat", "tm", None),),
        out_specs=P("tm", None),
        check_vma=False,
    )
```

time: 194 us -> 65.1 us (0.34)
  blocking collectives: 93.7 us -> 0 us
  Pallas kernels: 0 us -> 63 us
  other arithmetic: 32.3 us -> 0 us
  starting transfers between devices: 23.3 us -> 0 us
  local copies, waits for them, and re-layouts: 19.3 us -> 1.66 us
  matrix products: 16.7 us -> 0 us
  waiting for transfers between devices: 6.49 us -> 0 us
    pallas_call x0 -> x1, Pallas kernels: none -> 63 us  [local(): return call(fields).reshape(LOCAL, MONTHS)]
    psum x2 -> x0, blocking collectives: 55.6 us -> none  [one_axis_at_a_time(): return functools.reduce(lax.psum, axes, value)]
    all_to_all x2 -> x0, blocking collectives: 38 us -> none  [the longest x1 25.4 us: from_everyone(): lax.all_to_all(jnp.broadcast_to(value[None], (length, *value.shape)), axi...]
    all_to_all x2 -> x0, starting transfers between devices: 23.3 us -> none  [the longest x1 19.3 us: local(): lax.all_to_all(fourier, LAT, split_axis=0, concat_axis=1, tiled=True)]
    unnamed x24 -> x0, other arithmetic: 18.2 us -> none
    dot_general x2 -> x0, matrix products: 15.9 us -> none  [the longest x1 14.9 us: local(): lax.dot_general(transform, flat_fields, (((1,), (1,)), ((), ())), preferr...]
    all_to_all x2 -> x0, waiting for transfers between devices: 6.49 us -> none  [the longest x1 6.49 us: sum_at_owner(): lax.all_to_all(split_up(value, dim, length), axis, 0, 0, tiled=True)]
    another operation x5 -> x0, local copies, waits for them, and re-layouts: 5.94 us -> none  [the longest x1 5.02 us: legendre_blocks(): values = jnp.stack(outputs, axis=-1)]
  transfers between devices with their start and end apart: 2 -> 0, of which waited for: 1 -> 0; matrix products, arithmetic and copies ran while one was open for 19% -> 0% of each run, Pallas kernels for 0% -> 0%
where the time goes in v1:
time: 65.1 us; the launch traced here: 64.6 us
  Pallas kernels  63 us (97%)
  local copies, waits for them, and re-layouts  1.66 us (3%)
    pallas_call x1, Pallas kernels, local(): return call(fields).reshape(LOCAL, MONTHS)  63 us
    unnamed x3, local copies, waits for them, and re-layouts  1.66 us

profile of v1, /device:TPU:1, one launch (start us, length us, event | category | flops | bytes accessed | tf_op | source)
XLA Modules:
  0.0 64.6 jit_solution(10147110408852784419)
XLA Ops:
  0.0 0.0 copy-start
  0.0 1.0 %copy-done = bf16[8,32,1024]{2,1,0:T(8,128)(2,1)S(1)} copy-done((bf16[8,32,1024]{2,1,0:T(8,128)(2,1)S(1)}, bf16[8,32,1024]{2,1,0:T(8,128)(2,1)}, u32[]{:S(2)}) %copy-start) | copy-done | bytes 524312
  1.0 63.0 %shard_map.17 = f32[4,8,256]{2,1,0:T(8,128)S(1)} custom-call(bf16[8,32,1024]{2,1,0:T(8,128)(2,1)S(1)} %copy-done), custom_call_target="tpu_custom_call" | custom-call | tf_op jit(solution)/shard_map/pallas_call | solution.py:490
  64.0 0.6 copy.3
Async XLA Ops:
  0.0 1.0 %copy-start = (bf16[8,32,1024]{2,1,0:T(8,128)(2,1)S(1)}, bf16[8,32,1024]{2,1,0:T(8,128)(2,1)}, u32[]{:S(2)}) copy-start(bf16[8,32,1024]{2,1,0:T(8,128)(2,1)} %fields_hbm.1) | copy-start | bytes 1572868

commit v2 on v1

v2 whole, which is shorter than its diff:
```python
import functools
import math

import jax
import jax.numpy as jnp
from jax import lax
from jax.experimental import pallas as pl
from jax.experimental.pallas import tpu as pltpu
from jax.sharding import PartitionSpec as P

TRUNC = 341
NLON = 1024
NLAT = 512
MONTHS = 256
LATS = 64
TMS = 8
NX = 4
BLOCK = 8
LOCAL = 32
MIDDLE = 21
INNER = 22
OUTER = 42
DEPTH_OUT = (352, 272)
DEPTH_IN = (176, 144, 96, 48)
ROWS = 640
PART = ROWS // TMS
PITCH_OUT = 44
PITCH_IN = 24
KINDS = (
    (0, 9, 128, 0),
    (9, 14, 256, 0),
    (14, 16, 256, 128),
    (16, 17, 256, 256),
    (17, 18, 256, 384),
    (18, 32, 256, 512),
)
MESH = pl.DeviceIdType.MESH
F32 = jnp.float32
BF16 = jnp.bfloat16
SINE = tuple(
    (-1.0) ** k * (2.0 * math.pi) ** (2 * k + 1) / math.factorial(2 * k + 1) for k in range(7)
)


def sine_of_turns(u):
    square = u * u
    total = jnp.full_like(u, SINE[6])
    for k in range(5, -1, -1):
        total = total * square + SINE[k]
    return total * u


def cosine_of_phase(phase):
    away = jnp.abs(((phase + 512) & 1023) - 512)
    return sine_of_turns((256 - away).astype(F32) * (1.0 / NLON))


def waves_times_lon(first, slot_step, owner_step, part_step):
    sub = lax.broadcasted_iota(jnp.int32, (8, NLON), 0)
    lon = lax.broadcasted_iota(jnp.int32, (8, NLON), 1)
    wave = first + slot_step * ((sub >> 1) & 1) + owner_step * (sub >> 2)
    return wave * lon + part_step * (sub & 1)


def cosine_sine(phase):
    return cosine_of_phase(phase), cosine_of_phase(phase - 256)


def turn(pair, by):
    cosine, sine = pair
    return cosine * by[0] - sine * by[1], sine * by[0] + cosine * by[1]


def roll(value, shift, axis):
    return pltpu.roll(value, shift % value.shape[axis], axis)


def swap_bit(value, bit):
    rows = value.shape[0]
    sub = (lax.broadcasted_iota(jnp.int32, (rows, 128), 0) >> bit) & 1
    group = (lax.broadcasted_iota(jnp.int32, (rows, 128), 1) >> (5 + bit)) & 1
    step = 1 << bit
    from_below = roll(roll(value, 32 * step, 1), -step, 0)
    from_above = roll(roll(value, -32 * step, 1), step, 0)
    return jnp.where(sub == group, value, jnp.where(sub == 0, from_below, from_above))


def rows_by_latitude(spectrum):
    low, high = spectrum[:, :128], spectrum[:, 128:]
    return [swap_bit(swap_bit(part, 0), 1) for part in exchange_halves(low, high)]


def start_value(order, sine_lat):
    ratio = jnp.ones_like(order)
    for step in range(1, 9):
        ratio = ratio * ((order + step) / (order + (step + 0.5)))
    far = order + 9.0
    inverse = 1.0 / far
    square = inverse * inverse
    series = inverse * (-1.0 / 8.0 + square * (1.0 / 192.0 - square * (1.0 / 640.0)))
    log_ratio = 0.5 * jnp.log(far) + series + jnp.log(ratio)
    constant = math.log(0.5) - (0.5 * math.log(math.pi) - math.log(2.0))
    log_start = 0.5 * (constant + log_ratio) + order * jnp.log(sine_lat)
    taper = jnp.clip((log_start + 70.0) / 10.0, 0.0, 1.0)
    return jnp.exp(jnp.maximum(log_start, -80.0)) * taper


def step_factors(order, degree):
    top = jnp.sqrt((4.0 * degree * degree - 1.0) / (degree * degree - order * order))
    below = degree - 1.0
    back = jnp.sqrt(
        jnp.maximum(below * below - order * order, 0.0) / jnp.abs(4.0 * below * below - 1.0)
    )
    return top, top * back


def legendre(waves, lane_offset):
    place = (lax.broadcasted_iota(jnp.int32, (8, 128), 1) + lane_offset).astype(F32) + 0.5
    turns = place * (0.5 / NLAT)
    folded = jnp.minimum(turns, 0.5 - turns)
    half = sine_of_turns(0.5 * folded)
    cosine = jnp.where(folded < 0.125, 1.0 - 2.0 * half * half, sine_of_turns(0.25 - folded))
    return jnp.where(turns < 0.25, cosine, -cosine), sine_of_turns(folded)


def lat_weight(width):
    turns = (lax.broadcasted_iota(jnp.int32, (1, width), 1).astype(F32) + 0.5) * (0.5 / NLAT)
    return sine_of_turns(jnp.minimum(turns, 0.5 - turns)) * (math.pi / NLAT)


def regroup(pieces):
    group = lax.broadcasted_iota(jnp.int32, (PART, 128), 1) >> 5
    blocks = []
    for g in range(4):
        halves = []
        for half in range(2):
            total = None
            for a in range(4):
                moved = pieces[4 * half + a]
                if a != g:
                    moved = roll(moved, 32 * (a - g), 1)
                total = moved if total is None else jnp.where(group == a, moved, total)
            halves.append(total)
        blocks.append(jnp.concatenate(halves, axis=1))
    return jnp.concatenate(blocks, axis=0)


def exchange_halves(left, right):
    upper = ((lax.broadcasted_iota(jnp.int32, left.shape, 0) >> 2) & 1) == 0
    return (
        jnp.where(upper, left, roll(right, 4, 0)),
        jnp.where(upper, roll(left, -4, 0), right),
    )


def wrapped(value, length):
    return jnp.where(value >= length, value - length, value)


def is_inner(lat):
    return jnp.logical_and(lat >= MIDDLE, lat < MIDDLE + INNER)


def outer_owner(lat):
    return jnp.where(lat < MIDDLE, lat, lat - INNER)


def kernel(
    fields_hbm,
    out_ref,
    fields,
    patterns,
    transform,
    send_out,
    send_in,
    got,
    values,
    basis,
    coef,
    share,
    gram,
    slabs,
    planes,
    finals,
    local_sem,
    send_sem,
    row_sem,
    month_sem,
    slab_sem,
    plane_sem,
    last_sem,
):
    lat = lax.axis_index("lat")
    tm = lax.axis_index("tm")
    z = lat // NX
    x = lat % NX
    half = z % 2
    inner = is_inner(lat)
    outer = jnp.logical_not(inner)
    load = pltpu.make_async_copy(fields_hbm, fields, local_sem)
    load.start()
    got[...] = jnp.zeros_like(got)

    barrier = pltpu.get_barrier_semaphore()
    for away in range(32, 0, -1):
        for step in {away, LATS - away}:
            pl.semaphore_signal(
                barrier,
                inc=1,
                device_id={"lat": wrapped(lat + step, LATS)},
                device_id_type=MESH,
            )
    for step in range(1, TMS):
        pl.semaphore_signal(
            barrier, inc=1, device_id={"tm": wrapped(tm + step, TMS)}, device_id_type=MESH
        )

    for index in range(6):
        if index < 2:
            phase = waves_times_lon(2 * OUTER * index, OUTER, 0, 256)
        else:
            phase = waves_times_lon(168 + 2 * INNER * (index - 2), INNER, 0, 256)
        cosine, sine = cosine_sine(phase)
        patterns[2 * index] = cosine * (1.0 / math.sqrt(NLON))
        patterns[2 * index + 1] = sine * (1.0 / math.sqrt(NLON))
    by = cosine_sine(waves_times_lon(2, 0, 0, 0))

    def fill(kinds, trip, pair):
        following = turn(pair, by)
        for index in kinds:
            first = 176 * index if index < 2 else 352 + 96 * (index - 2)
            rows = [
                cosine * patterns[2 * index] - sine * patterns[2 * index + 1]
                for cosine, sine in (pair, following)
            ]
            start = pl.multiple_of(first + trip * 16, 16)
            transform[pl.ds(start, 16), :] = jnp.concatenate(rows, axis=0).astype(BF16)
        return turn(following, by)

    pair = cosine_sine(waves_times_lon(0, 0, 1, 0))
    pair = lax.fori_loop(0, 6, functools.partial(fill, range(6)), pair)
    lax.fori_loop(6, 11, functools.partial(fill, range(2)), pair)
    load.wait()
    flat = fields[...].reshape(BLOCK * LOCAL, NLON)
    for index in range(6):
        first, rows, buffer, place = (
            (176 * index, 176, send_out, index)
            if index < 2
            else (352 + 96 * (index - 2), 96, send_in, index - 2)
        )
        spectrum = lax.dot_general(
            transform[first : first + rows, :],
            flat,
            (((1,), (1,)), ((), ())),
            preferred_element_type=F32,
        )
        for odd, part in enumerate(rows_by_latitude(spectrum)):
            buffer[:, odd, :, place * 128 : (place + 1) * 128] = part.reshape(
                rows // 8, BLOCK, 128
            ).astype(BF16)

    own = jnp.where(inner, lat - MIDDLE, outer_owner(lat))

    @pl.when(inner)
    def _():
        got[lat] = send_in[own // 2, own % 2]

    @pl.when(outer)
    def _():
        got[lat, :, 0:256] = send_out[own // 2, own % 2]

    pl.semaphore_wait(barrier, LATS - 1 + TMS - 1)

    def row_copy(source, target, width, to_inner):
        if to_inner:
            peer = target - MIDDLE
            buffer = send_in
        else:
            peer = outer_owner(target)
            buffer = send_out
        return pltpu.make_async_remote_copy(
            src_ref=buffer.at[peer // 2, peer % 2, :, pl.ds(0, width)],
            dst_ref=got.at[source, :, pl.ds(0, width)],
            send_sem=send_sem.at[0],
            recv_sem=row_sem.at[source],
            device_id={"lat": target},
            device_id_type=MESH,
        )

    near = jnp.minimum(lat, LATS - 1 - lat)

    def each_row_copy(action):
        for lo, hi, width_out, width_in in KINDS:

            @pl.when(jnp.logical_and(near >= lo, near < hi))
            def _(width_out=width_out, width_in=width_in):
                def one(target):
                    to_inner = is_inner(target)

                    @pl.when(jnp.logical_not(to_inner))
                    def _():
                        action(row_copy(lat, target, width_out, False))

                    if width_in:

                        @pl.when(to_inner)
                        def _():
                            action(row_copy(lat, target, width_in, True))

                def both(step, carry):
                    one(wrapped(lat + (32 - step), LATS))
                    one(wrapped(lat + (32 + step), LATS))
                    return carry

                one(wrapped(lat + 32, LATS))
                lax.fori_loop(1, 32, both, 0)

    each_row_copy(lambda copy: copy.start())

    base = jnp.where(inner, 168, 0) + own
    stride = jnp.where(inner, INNER, OUTER)
    slot = jnp.minimum(
        lax.broadcasted_iota(jnp.int32, (8, 128), 0), jnp.where(inner, 7, 3)
    )
    order = (base + stride * slot).astype(F32)
    cosines = []
    state = []
    for block in range(4):
        cosine_lat, sine_lat = legendre(order, 128 * block)
        cosines.append(cosine_lat)
        first = start_value(order, sine_lat)
        values[block, 0:8, :] = first
        state.append(first)
        state.append(jnp.zeros_like(first))

    def advance(trip, carry):
        carry = list(carry)
        for step in range(1, 9):
            offset = trip * 8 + step
            top, mixed = step_factors(order, order + offset.astype(F32))
            row = pl.multiple_of(offset * 8, 8)
            for block in range(4):
                current, previous = carry[2 * block], carry[2 * block + 1]
                following = top * cosines[block] * current - mixed * previous
                values[block, pl.ds(row, 8), :] = following
                carry[2 * block], carry[2 * block + 1] = following, current
        return tuple(carry)

    lax.fori_loop(0, 44, advance, tuple(state))
    weight = lat_weight(NLAT)

    def tabulate(depths):
        for slot in range(2 * len(depths)):
            depth = depths[slot // 2]
            wave = base + stride * slot
            factor = jnp.where(wave > 0, math.sqrt(2.0), 1.0).astype(F32)
            offset = lax.broadcasted_iota(jnp.int32, (depth, 128), 0)
            for block in range(4):
                lanes = slice(128 * block, 128 * (block + 1))
                table = values[block, pl.ds(slot, depth, stride=8), :]
                table = jnp.where(
                    offset + wave <= TRUNC, table * (weight[:, lanes] * factor), 0.0
                )
                basis[slot, 0:depth, lanes] = table.astype(BF16)

    def receive(to_inner):
        for lo, hi, width_out, width_in in KINDS:
            width = width_in if to_inner else width_out
            if width:

                def one(source, carry, width=width):
                    @pl.when(source != lat)
                    def _():
                        row_copy(source, lat, width, to_inner).wait_recv()

                    return carry

                lax.fori_loop(lo, hi, one, 0)
                lax.fori_loop(LATS - hi, LATS - lo, one, 0)

    def combine(depths, narrow_from):
        first = 0
        for pair, depth in enumerate(depths):
            lo, hi = (16, 48) if pair >= narrow_from else (0, 64)
            data = got[lo:hi, :, pair * 128 : (pair + 1) * 128].astype(F32)
            data = data.reshape((hi - lo) * BLOCK, 128).astype(BF16)
            both = [
                lax.dot_general(
                    basis[2 * pair + side, 0:depth, lo * BLOCK : hi * BLOCK],
                    data,
                    (((1,), (0,)), ((), ())),
                    preferred_element_type=F32,
                )
                for side in range(2)
            ]
            lane = lax.broadcasted_iota(jnp.int32, (depth, 128), 1)
            coef[first : first + depth, :] = jnp.where(lane < 64, both[0], both[1]).astype(BF16)
            first += depth
        coef[first:ROWS, :] = jnp.zeros((ROWS - first, 128), BF16)

    @pl.when(outer)
    def _():
        tabulate(DEPTH_OUT)
        receive(False)
        combine(DEPTH_OUT, 2)

    @pl.when(inner)
    def _():
        tabulate(DEPTH_IN)
        receive(True)
        combine(DEPTH_IN, 2)

    def month_copy(source, target):
        return pltpu.make_async_remote_copy(
            src_ref=coef.at[pl.ds(pl.multiple_of(target * PART, PART), PART), :],
            dst_ref=share.at[source],
            send_sem=send_sem.at[1],
            recv_sem=month_sem.at[source],
            device_id={"tm": target},
            device_id_type=MESH,
        )

    for step in range(1, TMS):
        month_copy(tm, wrapped(tm + step, TMS)).start()
    share[tm] = coef[pl.ds(pl.multiple_of(tm * PART, PART), PART), :]
    for step in range(1, TMS):
        month_copy(wrapped(tm + step, TMS), tm).wait_recv()
    columns = regroup([share[source].astype(F32) for source in range(TMS)]).astype(BF16)
    terms = lax.dot_general(
        columns, columns, (((0,), (0,)), ((), ())), preferred_element_type=F32
    )
    row = lax.broadcasted_iota(jnp.int32, (MONTHS, MONTHS), 0)
    col = lax.broadcasted_iota(jnp.int32, (MONTHS, MONTHS), 1)
    diagonal = jnp.where(row == col, terms, 0.0)
    trace = jnp.sum(jnp.sum(diagonal, axis=0, keepdims=True), axis=1, keepdims=True)
    spare = jnp.logical_and((row & 3) == 1, col == row - 1)
    terms = jnp.where(spare, trace, terms)
    for odd, part in enumerate(exchange_halves(terms[:, :128], terms[:, 128:])):
        gram[:, odd] = part.reshape(32, 8, 128)

    me = tm * 8 + x * 2 + half

    def slab_copy(source, target):
        place = target % 8
        return pltpu.make_async_remote_copy(
            src_ref=gram.at[target // 2, target % 2],
            dst_ref=slabs.at[source],
            send_sem=send_sem.at[2],
            recv_sem=slab_sem.at[source],
            device_id={"lat": (z - half + place % 2) * NX + place // 2, "tm": target // 8},
            device_id_type=MESH,
        )

    def send_slab(step, carry):
        slab_copy(me, wrapped(me + step, 64)).start()
        return carry

    lax.fori_loop(1, 64, send_slab, 0)
    slabs[me] = gram[me // 2, me % 2]

    def receive_slab(step, carry):
        slab_copy(wrapped(me + step, 64), me).wait_recv()
        return carry

    lax.fori_loop(1, 64, receive_slab, 0)
    own_pair = z // 2
    planes[own_pair] = jnp.sum(slabs[...], axis=0)

    def plane_copy(source, target):
        return pltpu.make_async_remote_copy(
            src_ref=planes.at[own_pair],
            dst_ref=planes.at[source],
            send_sem=send_sem.at[3],
            recv_sem=plane_sem.at[source],
            device_id={"lat": (target * 2 + half) * NX + x},
            device_id_type=MESH,
        )

    for away in (4, 3, 5, 2, 6, 1, 7):
        plane_copy(own_pair, wrapped(own_pair + away, 8)).start()

    each_row_copy(lambda copy: copy.wait_send())
    for step in range(1, TMS):
        month_copy(tm, wrapped(tm + step, TMS)).wait_send()

    def slab_sent(step, carry):
        slab_copy(me, wrapped(me + step, 64)).wait_send()
        return carry

    lax.fori_loop(1, 64, slab_sent, 0)

    for away in range(1, 8):
        plane_copy(wrapped(own_pair + away, 8), own_pair).wait_recv()
    slab = jnp.sum(planes[...], axis=0)
    later = me // 32
    row = lax.broadcasted_iota(jnp.int32, (8, 128), 0) - 4 * later
    col = lax.broadcasted_iota(jnp.int32, (8, 128), 1) - (4 * me - 128 * later)
    spare = jnp.logical_and(row == 1, col == 0)
    twin = jnp.logical_and(row == 0, col == 1)

    def pick(mask):
        chosen = jnp.sum(jnp.where(mask, slab, 0.0), axis=0, keepdims=True)
        return jnp.sum(chosen, axis=1, keepdims=True)

    total = pick(spare)
    place = x * 2 + half
    finals[place] = jnp.where(spare, pick(twin), slab) * (MONTHS / (total + 1e-06))

    def last_copy(source, target):
        return pltpu.make_async_remote_copy(
            src_ref=finals.at[place],
            dst_ref=finals.at[source],
            send_sem=send_sem.at[4],
            recv_sem=last_sem.at[source],
            device_id={"lat": (z - half + target % 2) * NX + target // 2},
            device_id_type=MESH,
        )

    for away in (4, 5, 3, 2, 6, 1, 7):
        last_copy(place, wrapped(place + away, 8)).start()
    for away in range(1, 8):
        plane_copy(own_pair, wrapped(own_pair + away, 8)).wait_send()
    for away in range(1, 8):
        last_copy(wrapped(place + away, 8), place).wait_recv()
    for index in range(4):
        left, right = exchange_halves(finals[2 * index], finals[2 * index + 1])
        out_ref[8 * index : 8 * (index + 1), 0:128] = left
        out_ref[8 * index : 8 * (index + 1), 128:256] = right
    for away in range(1, 8):
        last_copy(place, wrapped(place + away, 8)).wait_send()


def local(fields):
    return pl.pallas_call(
        kernel,
        out_shape=jax.ShapeDtypeStruct((LOCAL, MONTHS), F32),
        in_specs=[pl.BlockSpec(memory_space=pltpu.HBM)],
        out_specs=pl.BlockSpec(memory_space=pltpu.VMEM),
        scratch_shapes=[
            pltpu.VMEM((BLOCK, LOCAL, NLON), BF16),
            pltpu.VMEM((12, 8, NLON), F32),
            pltpu.VMEM((736, NLON), BF16),
            pltpu.VMEM((PITCH_OUT // 2, 2, BLOCK, 256), BF16),
            pltpu.VMEM((PITCH_IN // 2, 2, BLOCK, 512), BF16),
            pltpu.VMEM((LATS, BLOCK, 512), BF16),
            pltpu.VMEM((4, 353 * 8, 128), F32),
            pltpu.VMEM((8, 352, NLAT), BF16),
            pltpu.VMEM((ROWS, 128), BF16),
            pltpu.VMEM((TMS, PART, 128), BF16),
            pltpu.VMEM((32, 2, 8, 128), F32),
            pltpu.VMEM((64, 8, 128), F32),
            pltpu.VMEM((8, 8, 128), F32),
            pltpu.VMEM((8, 8, 128), F32),
            pltpu.SemaphoreType.DMA,
            pltpu.SemaphoreType.DMA((5,)),
            pltpu.SemaphoreType.DMA((LATS,)),
            pltpu.SemaphoreType.DMA((TMS,)),
            pltpu.SemaphoreType.DMA((64,)),
            pltpu.SemaphoreType.DMA((8,)),
            pltpu.SemaphoreType.DMA((8,)),
        ],
        compiler_params=pltpu.CompilerParams(
            collective_id=0, has_side_effects=True, vmem_limit_bytes=67_043_328
        ),
    )(fields)


def solution(mesh):
    return jax.shard_map(
        local,
        mesh=mesh,
        in_specs=(P("lat", "tm", None),),
        out_specs=P("tm", None),
        check_vma=False,
    )
```

time: 65.1 us -> 59 us (0.906)
  Pallas kernels: 63 us -> 57.3 us
    pallas_call x1, Pallas kernels: 63 us -> 57.3 us  [local(): pl.pallas_call(kernel, out_shape=jax.ShapeDtypeStruct((LOCAL, MONTHS), F3...]
    unnamed x3 -> x1, local copies, waits for them, and re-layouts: 1.66 us -> 1.38 us
where the time goes in v2:
time: 59 us; the launch traced here: 58.7 us
  Pallas kernels  57.3 us (97%)
  local copies, waits for them, and re-layouts  1.38 us (2%)
    pallas_call x1, Pallas kernels, local(): pl.pallas_call(kernel, out_shape=jax.ShapeDtypeStruct((LOCAL, MONTHS), F3...  57.3 us
    unnamed x1, local copies, waits for them, and re-layouts  1.38 us

profile of v2, /device:TPU:1, one launch (start us, length us, event | category | flops | bytes accessed | tf_op | source)
XLA Modules:
  0.0 58.7 jit_solution(17611647444330311730)
XLA Ops:
  0.0 57.3 %shard_map.17 = f32[32,256]{1,0:T(8,128)} custom-call(bf16[8,32,1024]{2,1,0:T(8,128)(2,1)} %fields_hbm.1), custom_call_target="tpu_custom_call" | custom-call | tf_op jit(solution)/shard_map/pallas_call | solution.py:534
  57.3 1.4 %copy.3 = f32[32,256]{1,0:T(8,128)} copy(f32[32,256]{1,0:T(8,128)} %shard_map.17) | data formatting | bytes 65536

commit v3 on v2

--- a/solution.py
+++ b/solution.py
@@ -22,8 +22,8 @@
 OUTER = 42
 DEPTH_OUT = (352, 272)
 DEPTH_IN = (176, 144, 96, 48)
-ROWS = 640
-PART = ROWS // TMS
+PART_OUT = 80
+PART_IN = 64
 PITCH_OUT = 44
 PITCH_IN = 24
 KINDS = (
@@ -129,7 +129,7 @@
 
 
 def regroup(pieces):
-    group = lax.broadcasted_iota(jnp.int32, (PART, 128), 1) >> 5
+    group = lax.broadcasted_iota(jnp.int32, pieces[0].shape, 1) >> 5
     blocks = []
     for g in range(4):
         halves = []
@@ -378,10 +378,10 @@
                 lax.fori_loop(lo, hi, one, 0)
                 lax.fori_loop(LATS - hi, LATS - lo, one, 0)
 
-    def combine(depths, narrow_from):
+    def combine(depths, rows):
         first = 0
         for pair, depth in enumerate(depths):
-            lo, hi = (16, 48) if pair >= narrow_from else (0, 64)
+            lo, hi = (16, 48) if pair >= 2 else (0, 64)
             data = got[lo:hi, :, pair * 128 : (pair + 1) * 128].astype(F32)
             data = data.reshape((hi - lo) * BLOCK, 128).astype(BF16)
             both = [
@@ -396,73 +396,89 @@
             lane = lax.broadcasted_iota(jnp.int32, (depth, 128), 1)
             coef[first : first + depth, :] = jnp.where(lane < 64, both[0], both[1]).astype(BF16)
             first += depth
-        coef[first:ROWS, :] = jnp.zeros((ROWS - first, 128), BF16)
+        coef[first:rows, :] = jnp.zeros((rows - first, 128), BF16)
+
+    def month_copy(source, target, part):
+        return pltpu.make_async_remote_copy(
+            src_ref=coef.at[pl.ds(pl.multiple_of(target * part, part), part), :],
+            dst_ref=share.at[source, pl.ds(0, part), :],
+            send_sem=send_sem.at[1],
+            recv_sem=month_sem.at[source],
+            device_id={"tm": target},
+            device_id_type=MESH,
+        )
+
+    def months(part):
+        steps = (4, 3, 5, 2, 6, 1, 7)
+        for step in steps:
+            month_copy(tm, wrapped(tm + step, TMS), part).start()
+        share[tm, 0:part, :] = coef[pl.ds(pl.multiple_of(tm * part, part), part), :]
+        for step in steps[::-1]:
+            month_copy(wrapped(tm + step, TMS), tm, part).wait_recv()
+        pieces = [share[source, 0:part, :].astype(F32) for source in range(TMS)]
+        columns = regroup(pieces).astype(BF16)
+        terms = lax.dot_general(
+            columns, columns, (((0,), (0,)), ((), ())), preferred_element_type=F32
+        )
+        row = lax.broadcasted_iota(jnp.int32, (MONTHS, MONTHS), 0)
+        col = lax.broadcasted_iota(jnp.int32, (MONTHS, MONTHS), 1)
+        diagonal = jnp.where(row == col, terms, 0.0)
+        trace = jnp.sum(jnp.sum(diagonal, axis=0, keepdims=True), axis=1, keepdims=True)
+        spare = jnp.logical_and((row & 3) == 1, col == row - 1)
+        terms = jnp.where(spare, trace, terms)
+        for odd, value in enumerate(exchange_halves(terms[:, :128], terms[:, 128:])):
+            gram[:, odd] = value.reshape(32, 8, 128)
 
     @pl.when(outer)
     def _():
         tabulate(DEPTH_OUT)
         receive(False)
-        combine(DEPTH_OUT, 2)
+        combine(DEPTH_OUT, TMS * PART_OUT)
+        months(PART_OUT)
 
     @pl.when(inner)
     def _():
         tabulate(DEPTH_IN)
         receive(True)
-        combine(DEPTH_IN, 2)
-
-    def month_copy(source, target):
+        combine(DEPTH_IN, TMS * PART_IN)
+        months(PART_IN)
+
+    me = tm * 8 + x * 2 + half
+    y = tm // 2
+    core = tm % 2
+    plane = (z - half) * NX
+
+    def slab_copy(source, target_y, target_core, target_x, target_half):
+        target = target_y * 2 + target_core
         return pltpu.make_async_remote_copy(
-            src_ref=coef.at[pl.ds(pl.multiple_of(target * PART, PART), PART), :],
-            dst_ref=share.at[source],
-            send_sem=send_sem.at[1],
-            recv_sem=month_sem.at[source],
-            device_id={"tm": target},
-            device_id_type=MESH,
-        )
-
-    for step in range(1, TMS):
-        month_copy(tm, wrapped(tm + step, TMS)).start()
-    share[tm] = coef[pl.ds(pl.multiple_of(tm * PART, PART), PART), :]
-    for step in range(1, TMS):
-        month_copy(wrapped(tm + step, TMS), tm).wait_recv()
-    columns = regroup([share[source].astype(F32) for source in range(TMS)]).astype(BF16)
-    terms = lax.dot_general(
-        columns, columns, (((0,), (0,)), ((), ())), preferred_element_type=F32
-    )
-    row = lax.broadcasted_iota(jnp.int32, (MONTHS, MONTHS), 0)
-    col = lax.broadcasted_iota(jnp.int32, (MONTHS, MONTHS), 1)
-    diagonal = jnp.where(row == col, terms, 0.0)
-    trace = jnp.sum(jnp.sum(diagonal, axis=0, keepdims=True), axis=1, keepdims=True)
-    spare = jnp.logical_and((row & 3) == 1, col == row - 1)
-    terms = jnp.where(spare, trace, terms)
-    for odd, part in enumerate(exchange_halves(terms[:, :128], terms[:, 128:])):
-        gram[:, odd] = part.reshape(32, 8, 128)
-
-    me = tm * 8 + x * 2 + half
-
-    def slab_copy(source, target):
-        place = target % 8
-        return pltpu.make_async_remote_copy(
-            src_ref=gram.at[target // 2, target % 2],
+            src_ref=gram.at[target * NX + target_x, target_half],
             dst_ref=slabs.at[source],
             send_sem=send_sem.at[2],
             recv_sem=slab_sem.at[source],
-            device_id={"lat": (z - half + place % 2) * NX + place // 2, "tm": target // 8},
+            device_id={"lat": plane + target_half * NX + target_x, "tm": target},
             device_id_type=MESH,
         )
 
-    def send_slab(step, carry):
-        slab_copy(me, wrapped(me + step, 64)).start()
-        return carry
-
-    lax.fori_loop(1, 64, send_slab, 0)
+    def others(away_first, action):
+        order = (2, 1, 3, 0)
+        for away_y in order if away_first else order[::-1]:
+            peer_y = wrapped(y + away_y, 4)
+            for away_x in order if away_first else order[::-1]:
+                peer_x = wrapped(x + away_x, 4)
+                for peer_half in (1 - half, half) if away_first else (half, 1 - half):
+                    for peer_core in (1 - core, core):
+                        here = away_y == 0 and away_x == 0
+                        if not (here and peer_half is half and peer_core is core):
+                            action(peer_y, peer_core, peer_x, peer_half)
+
+    others(True, lambda *peer: slab_copy(me, *peer).start())
     slabs[me] = gram[me // 2, me % 2]
 
-    def receive_slab(step, carry):
-        slab_copy(wrapped(me + step, 64), me).wait_recv()
-        return carry
-
-    lax.fori_loop(1, 64, receive_slab, 0)
+    def receive_slab(peer_y, peer_core, peer_x, peer_half):
+        source = (peer_y * 2 + peer_core) * 8 + peer_x * 2 + peer_half
+        slab_copy(source, y, core, x, half).wait_recv()
+
+    others(False, receive_slab)
     own_pair = z // 2
     planes[own_pair] = jnp.sum(slabs[...], axis=0)
 
@@ -480,11 +496,15 @@
         plane_copy(own_pair, wrapped(own_pair + away, 8)).start()
 
     each_row_copy(lambda copy: copy.wait_send())
-    for step in range(1, TMS):
-        month_copy(tm, wrapped(tm + step, TMS)).wait_send()
+    for applies, part in ((outer, PART_OUT), (inner, PART_IN)):
+
+        @pl.when(applies)
+        def _(part=part):
+            for step in range(1, TMS):
+                month_copy(tm, wrapped(tm + step, TMS), part).wait_send()
 
     def slab_sent(step, carry):
-        slab_copy(me, wrapped(me + step, 64)).wait_send()
+        slab_copy(me, y, core, x, half).wait_send()
         return carry
 
     lax.fori_loop(1, 64, slab_sent, 0)
@@ -545,8 +565,8 @@
             pltpu.VMEM((LATS, BLOCK, 512), BF16),
             pltpu.VMEM((4, 353 * 8, 128), F32),
             pltpu.VMEM((8, 352, NLAT), BF16),
-            pltpu.VMEM((ROWS, 128), BF16),
-            pltpu.VMEM((TMS, PART, 128), BF16),
+            pltpu.VMEM((TMS * PART_OUT, 128), BF16),
+            pltpu.VMEM((TMS, PART_OUT, 128), BF16),
             pltpu.VMEM((32, 2, 8, 128), F32),
             pltpu.VMEM((64, 8, 128), F32),
             pltpu.VMEM((8, 8, 128), F32),

time: 59 us -> 57.9 us (0.981)
  Pallas kernels: 57.3 us -> 56.1 us
    pallas_call x1, Pallas kernels: 57.3 us -> 56.1 us  [local(): pl.pallas_call(kernel, out_shape=jax.ShapeDtypeStruct((LOCAL, MONTHS), F3...]
where the time goes in v3:
time: 57.9 us; the launch traced here: 57.4 us
  Pallas kernels  56.1 us (97%)
  local copies, waits for them, and re-layouts  1.38 us (2%)
    pallas_call x1, Pallas kernels, local(): pl.pallas_call(kernel, out_shape=jax.ShapeDtypeStruct((LOCAL, MONTHS), F3...  56.1 us
    unnamed x1, local copies, waits for them, and re-layouts  1.38 us

profile of v3, /device:TPU:1, one launch (start us, length us, event | category | flops | bytes accessed | tf_op | source)
XLA Modules:
  0.0 57.4 jit_solution(4717838893303750713)
XLA Ops:
  0.0 56.1 %shard_map.17 = f32[32,256]{1,0:T(8,128)} custom-call(bf16[8,32,1024]{2,1,0:T(8,128)(2,1)} %fields_hbm.1), custom_call_target="tpu_custom_call" | custom-call | tf_op jit(solution)/shard_map/pallas_call | solution.py:554
  56.1 1.4 %copy.3 = f32[32,256]{1,0:T(8,128)} copy(f32[32,256]{1,0:T(8,128)} %shard_map.17) | data formatting | bytes 65536

commit v4 on v3

--- a/solution.py
+++ b/solution.py
@@ -17,7 +17,7 @@
 NX = 4
 BLOCK = 8
 LOCAL = 32
-MIDDLE = 21
+MIDDLE = 19
 INNER = 22
 OUTER = 42
 DEPTH_OUT = (352, 272)
@@ -382,8 +382,8 @@
         first = 0
         for pair, depth in enumerate(depths):
             lo, hi = (16, 48) if pair >= 2 else (0, 64)
-            data = got[lo:hi, :, pair * 128 : (pair + 1) * 128].astype(F32)
-            data = data.reshape((hi - lo) * BLOCK, 128).astype(BF16)
+            data = got[lo:hi, :, pair * 128 : (pair + 1) * 128]
+            data = data.reshape((hi - lo) * BLOCK, 128)
             both = [
                 lax.dot_general(
                     basis[2 * pair + side, 0:depth, lo * BLOCK : hi * BLOCK],
@@ -422,8 +422,8 @@
         )
         row = lax.broadcasted_iota(jnp.int32, (MONTHS, MONTHS), 0)
         col = lax.broadcasted_iota(jnp.int32, (MONTHS, MONTHS), 1)
-        diagonal = jnp.where(row == col, terms, 0.0)
-        trace = jnp.sum(jnp.sum(diagonal, axis=0, keepdims=True), axis=1, keepdims=True)
+        squares = functools.reduce(jnp.add, [piece * piece for piece in pieces])
+        trace = jnp.sum(jnp.sum(squares, axis=0, keepdims=True), axis=1, keepdims=True)
         spare = jnp.logical_and((row & 3) == 1, col == row - 1)
         terms = jnp.where(spare, trace, terms)
         for odd, value in enumerate(exchange_halves(terms[:, :128], terms[:, 128:])):
@@ -516,15 +516,9 @@
     row = lax.broadcasted_iota(jnp.int32, (8, 128), 0) - 4 * later
     col = lax.broadcasted_iota(jnp.int32, (8, 128), 1) - (4 * me - 128 * later)
     spare = jnp.logical_and(row == 1, col == 0)
-    twin = jnp.logical_and(row == 0, col == 1)
-
-    def pick(mask):
-        chosen = jnp.sum(jnp.where(mask, slab, 0.0), axis=0, keepdims=True)
-        return jnp.sum(chosen, axis=1, keepdims=True)
-
-    total = pick(spare)
+
     place = x * 2 + half
-    finals[place] = jnp.where(spare, pick(twin), slab) * (MONTHS / (total + 1e-06))
+    finals[place] = jnp.where(spare, roll(roll(slab, 1, 0), -1, 1), slab)
 
     def last_copy(source, target):
         return pltpu.make_async_remote_copy(
@@ -540,12 +534,14 @@
         last_copy(place, wrapped(place + away, 8)).start()
     for away in range(1, 8):
         plane_copy(own_pair, wrapped(own_pair + away, 8)).wait_send()
+    chosen = jnp.sum(jnp.where(spare, slab, 0.0), axis=0, keepdims=True)
+    scale = MONTHS / (jnp.sum(chosen, axis=1, keepdims=True) + 1e-06)
     for away in range(1, 8):
         last_copy(wrapped(place + away, 8), place).wait_recv()
     for index in range(4):
         left, right = exchange_halves(finals[2 * index], finals[2 * index + 1])
-        out_ref[8 * index : 8 * (index + 1), 0:128] = left
-        out_ref[8 * index : 8 * (index + 1), 128:256] = right
+        out_ref[8 * index : 8 * (index + 1), 0:128] = left * scale
+        out_ref[8 * index : 8 * (index + 1), 128:256] = right * scale
     for away in range(1, 8):
         last_copy(place, wrapped(place + away, 8)).wait_send()
 

time: 57.9 us -> 57.1 us (0.986)
  no operation moved by 1% of the time
where the time goes in v4:
time: 57.1 us; the launch traced here: 56.9 us
  Pallas kernels  55.6 us (97%)
  local copies, waits for them, and re-layouts  1.38 us (2%)
    pallas_call x1, Pallas kernels, local(): pl.pallas_call(kernel, out_shape=jax.ShapeDtypeStruct((LOCAL, MONTHS), F3...  55.6 us
    unnamed x1, local copies, waits for them, and re-layouts  1.38 us

profile of v4, /device:TPU:1, one launch (start us, length us, event | category | flops | bytes accessed | tf_op | source)
XLA Modules:
  0.0 56.9 jit_solution(13978859525394782951)
XLA Ops:
  0.0 55.6 %shard_map.17 = f32[32,256]{1,0:T(8,128)} custom-call(bf16[8,32,1024]{2,1,0:T(8,128)(2,1)} %fields_hbm.1), custom_call_target="tpu_custom_call" | custom-call | tf_op jit(solution)/shard_map/pallas_call | solution.py:550
  55.6 1.4 %copy.3 = f32[32,256]{1,0:T(8,128)} copy(f32[32,256]{1,0:T(8,128)} %shard_map.17) | data formatting | bytes 65536

commit v5 on v4

--- a/solution.py
+++ b/solution.py
@@ -17,22 +17,27 @@
 NX = 4
 BLOCK = 8
 LOCAL = 32
-MIDDLE = 19
-INNER = 22
-OUTER = 42
-DEPTH_OUT = (352, 272)
-DEPTH_IN = (176, 144, 96, 48)
+MIDDLE = 23
+INNER = 16
+IDLE = 2
+OUTER = 46
+FIRST_IN = 4 * OUTER
+DEPTH_OUT = (352, 256)
+DEPTH_IN = (160, 128, 96, 64, 32)
 PART_OUT = 80
 PART_IN = 64
-PITCH_OUT = 44
-PITCH_IN = 24
+PITCH_OUT = 48
+PITCH_IN = 16
+PAIRS_OUT = len(DEPTH_OUT)
+PAIRS = PAIRS_OUT + len(DEPTH_IN)
+LANES_IN = 128 * len(DEPTH_IN)
 KINDS = (
     (0, 9, 128, 0),
-    (9, 14, 256, 0),
-    (14, 16, 256, 128),
+    (9, 15, 256, 0),
+    (15, 16, 256, 128),
     (16, 17, 256, 256),
     (17, 18, 256, 384),
-    (18, 32, 256, 512),
+    (18, 32, 256, 640),
 )
 MESH = pl.DeviceIdType.MESH
 F32 = jnp.float32
@@ -80,8 +85,10 @@
     sub = (lax.broadcasted_iota(jnp.int32, (rows, 128), 0) >> bit) & 1
     group = (lax.broadcasted_iota(jnp.int32, (rows, 128), 1) >> (5 + bit)) & 1
     step = 1 << bit
-    from_below = roll(roll(value, 32 * step, 1), -step, 0)
-    from_above = roll(roll(value, -32 * step, 1), step, 0)
+    down = roll(value, 32 * step, 1)
+    up = down if step == 2 else roll(value, -32 * step, 1)
+    from_below = roll(down, -step, 0)
+    from_above = roll(up, step, 0)
     return jnp.where(sub == group, value, jnp.where(sub == 0, from_below, from_above))
 
 
@@ -161,8 +168,18 @@
     return jnp.logical_and(lat >= MIDDLE, lat < MIDDLE + INNER)
 
 
+def is_outer(lat):
+    return jnp.logical_or(lat < MIDDLE, lat >= MIDDLE + INNER + IDLE)
+
+
 def outer_owner(lat):
-    return jnp.where(lat < MIDDLE, lat, lat - INNER)
+    return jnp.where(lat < MIDDLE, lat, lat - INNER - IDLE)
+
+
+def pair_rows(index):
+    if index < PAIRS_OUT:
+        return 4 * PITCH_OUT * index, 4 * PITCH_OUT
+    return 4 * (PITCH_OUT * PAIRS_OUT + PITCH_IN * (index - PAIRS_OUT)), 4 * PITCH_IN
 
 
 def kernel(
@@ -175,6 +192,7 @@
     send_in,
     got,
     values,
+    more_values,
     basis,
     coef,
     share,
@@ -196,7 +214,7 @@
     x = lat % NX
     half = z % 2
     inner = is_inner(lat)
-    outer = jnp.logical_not(inner)
+    outer = is_outer(lat)
     load = pltpu.make_async_copy(fields_hbm, fields, local_sem)
     load.start()
     got[...] = jnp.zeros_like(got)
@@ -215,11 +233,12 @@
             barrier, inc=1, device_id={"tm": wrapped(tm + step, TMS)}, device_id_type=MESH
         )
 
-    for index in range(6):
-        if index < 2:
+    for index in range(PAIRS):
+        if index < PAIRS_OUT:
             phase = waves_times_lon(2 * OUTER * index, OUTER, 0, 256)
         else:
-            phase = waves_times_lon(168 + 2 * INNER * (index - 2), INNER, 0, 256)
+            first = FIRST_IN + 2 * INNER * (index - PAIRS_OUT)
+            phase = waves_times_lon(first, INNER, 0, 256)
         cosine, sine = cosine_sine(phase)
         patterns[2 * index] = cosine * (1.0 / math.sqrt(NLON))
         patterns[2 * index + 1] = sine * (1.0 / math.sqrt(NLON))
@@ -228,7 +247,7 @@
     def fill(kinds, trip, pair):
         following = turn(pair, by)
         for index in kinds:
-            first = 176 * index if index < 2 else 352 + 96 * (index - 2)
+            first, _ = pair_rows(index)
             rows = [
                 cosine * patterns[2 * index] - sine * patterns[2 * index + 1]
                 for cosine, sine in (pair, following)
@@ -238,16 +257,17 @@
         return turn(following, by)
 
     pair = cosine_sine(waves_times_lon(0, 0, 1, 0))
-    pair = lax.fori_loop(0, 6, functools.partial(fill, range(6)), pair)
-    lax.fori_loop(6, 11, functools.partial(fill, range(2)), pair)
+    trips_in, trips_out = PITCH_IN // 4, PITCH_OUT // 4
+    pair = lax.fori_loop(0, trips_in, functools.partial(fill, range(PAIRS)), pair)
+    lax.fori_loop(trips_in, trips_out, functools.partial(fill, range(PAIRS_OUT)), pair)
     load.wait()
     flat = fields[...].reshape(BLOCK * LOCAL, NLON)
-    for index in range(6):
-        first, rows, buffer, place = (
-            (176 * index, 176, send_out, index)
-            if index < 2
-            else (352 + 96 * (index - 2), 96, send_in, index - 2)
-        )
+    for index in range(PAIRS):
+        first, rows = pair_rows(index)
+        if index < PAIRS_OUT:
+            buffer, place = send_out, index
+        else:
+            buffer, place = send_in, index - PAIRS_OUT
         spectrum = lax.dot_general(
             transform[first : first + rows, :],
             flat,
@@ -297,7 +317,7 @@
                 def one(target):
                     to_inner = is_inner(target)
 
-                    @pl.when(jnp.logical_not(to_inner))
+                    @pl.when(is_outer(target))
                     def _():
                         action(row_copy(lat, target, width_out, False))
 
@@ -317,36 +337,45 @@
 
     each_row_copy(lambda copy: copy.start())
 
-    base = jnp.where(inner, 168, 0) + own
+    base = jnp.where(inner, FIRST_IN + own, jnp.where(outer, own, 400))
     stride = jnp.where(inner, INNER, OUTER)
     slot = jnp.minimum(
         lax.broadcasted_iota(jnp.int32, (8, 128), 0), jnp.where(inner, 7, 3)
     )
     order = (base + stride * slot).astype(F32)
-    cosines = []
-    state = []
-    for block in range(4):
-        cosine_lat, sine_lat = legendre(order, 128 * block)
-        cosines.append(cosine_lat)
-        first = start_value(order, sine_lat)
-        values[block, 0:8, :] = first
-        state.append(first)
-        state.append(jnp.zeros_like(first))
-
-    def advance(trip, carry):
-        carry = list(carry)
-        for step in range(1, 9):
-            offset = trip * 8 + step
-            top, mixed = step_factors(order, order + offset.astype(F32))
-            row = pl.multiple_of(offset * 8, 8)
-            for block in range(4):
-                current, previous = carry[2 * block], carry[2 * block + 1]
-                following = top * cosines[block] * current - mixed * previous
-                values[block, pl.ds(row, 8), :] = following
-                carry[2 * block], carry[2 * block + 1] = following, current
-        return tuple(carry)
-
-    lax.fori_loop(0, 44, advance, tuple(state))
+    def recur(order, table, trips):
+        cosines = []
+        state = []
+        for block in range(4):
+            cosine_lat, sine_lat = legendre(order, 128 * block)
+            cosines.append(cosine_lat)
+            first = start_value(order, sine_lat)
+            table[block, 0:8, :] = first
+            state.append(first)
+            state.append(jnp.zeros_like(first))
+
+        def advance(trip, carry):
+            carry = list(carry)
+            for step in range(1, 9):
+                offset = trip * 8 + step
+                top, mixed = step_factors(order, order + offset.astype(F32))
+                row = pl.multiple_of(offset * 8, 8)
+                for block in range(4):
+                    current, previous = carry[2 * block], carry[2 * block + 1]
+                    following = top * cosines[block] * current - mixed * previous
+                    table[block, pl.ds(row, 8), :] = following
+                    carry[2 * block], carry[2 * block + 1] = following, current
+            return tuple(carry)
+
+        lax.fori_loop(0, trips, advance, tuple(state))
+
+    recur(order, values, 44)
+
+    @pl.when(inner)
+    def _():
+        slot = 8 + jnp.minimum(lax.broadcasted_iota(jnp.int32, (8, 128), 0), 1)
+        recur((base + stride * slot).astype(F32), more_values, 4)
+
     weight = lat_weight(NLAT)
 
     def tabulate(depths):
@@ -357,7 +386,8 @@
             offset = lax.broadcasted_iota(jnp.int32, (depth, 128), 0)
             for block in range(4):
                 lanes = slice(128 * block, 128 * (block + 1))
-                table = values[block, pl.ds(slot, depth, stride=8), :]
+                source = values if slot < 8 else more_values
+                table = source[block, pl.ds(slot % 8, depth, stride=8), :]
                 table = jnp.where(
                     offset + wave <= TRUNC, table * (weight[:, lanes] * factor), 0.0
                 )
@@ -381,7 +411,7 @@
     def combine(depths, rows):
         first = 0
         for pair, depth in enumerate(depths):
-            lo, hi = (16, 48) if pair >= 2 else (0, 64)
+            lo, hi = (16, 48) if pair >= 1 and len(depths) > 2 else (0, 64)
             data = got[lo:hi, :, pair * 128 : (pair + 1) * 128]
             data = data.reshape((hi - lo) * BLOCK, 128)
             both = [
@@ -429,10 +459,14 @@
         for odd, value in enumerate(exchange_halves(terms[:, :128], terms[:, 128:])):
             gram[:, odd] = value.reshape(32, 8, 128)
 
-    @pl.when(outer)
+    @pl.when(jnp.logical_not(inner))
     def _():
         tabulate(DEPTH_OUT)
-        receive(False)
+
+        @pl.when(outer)
+        def _():
+            receive(False)
+
         combine(DEPTH_OUT, TMS * PART_OUT)
         months(PART_OUT)
 
@@ -496,7 +530,7 @@
         plane_copy(own_pair, wrapped(own_pair + away, 8)).start()
 
     each_row_copy(lambda copy: copy.wait_send())
-    for applies, part in ((outer, PART_OUT), (inner, PART_IN)):
+    for applies, part in ((jnp.logical_not(inner), PART_OUT), (inner, PART_IN)):
 
         @pl.when(applies)
         def _(part=part):
@@ -554,13 +588,14 @@
         out_specs=pl.BlockSpec(memory_space=pltpu.VMEM),
         scratch_shapes=[
             pltpu.VMEM((BLOCK, LOCAL, NLON), BF16),
-            pltpu.VMEM((12, 8, NLON), F32),
-            pltpu.VMEM((736, NLON), BF16),
+            pltpu.VMEM((2 * PAIRS, 8, NLON), F32),
+            pltpu.VMEM((sum(pair_rows(PAIRS - 1)), NLON), BF16),
             pltpu.VMEM((PITCH_OUT // 2, 2, BLOCK, 256), BF16),
-            pltpu.VMEM((PITCH_IN // 2, 2, BLOCK, 512), BF16),
-            pltpu.VMEM((LATS, BLOCK, 512), BF16),
+            pltpu.VMEM((PITCH_IN // 2, 2, BLOCK, LANES_IN), BF16),
+            pltpu.VMEM((LATS, BLOCK, LANES_IN), BF16),
             pltpu.VMEM((4, 353 * 8, 128), F32),
-            pltpu.VMEM((8, 352, NLAT), BF16),
+            pltpu.VMEM((4, 33 * 8, 128), F32),
+            pltpu.VMEM((10, 352, NLAT), BF16),
             pltpu.VMEM((TMS * PART_OUT, 128), BF16),
             pltpu.VMEM((TMS, PART_OUT, 128), BF16),
             pltpu.VMEM((32, 2, 8, 128), F32),

time: 57.1 us -> 56.7 us (level)
  no operation moved by 1% of the time
where the time goes in v5:
time: 56.7 us; the launch traced here: 56.6 us
  Pallas kernels  55.2 us (97%)
  local copies, waits for them, and re-layouts  1.38 us (2%)
    pallas_call x1, Pallas kernels, local(): pl.pallas_call(kernel, out_shape=jax.ShapeDtypeStruct((LOCAL, MONTHS), F3...  55.2 us
    unnamed x1, local copies, waits for them, and re-layouts  1.38 us

profile of v5, /device:TPU:1, one launch (start us, length us, event | category | flops | bytes accessed | tf_op | source)
XLA Modules:
  0.0 56.6 jit_solution(4021830771165413999)
XLA Ops:
  0.0 55.2 %shard_map.17 = f32[32,256]{1,0:T(8,128)} custom-call(bf16[8,32,1024]{2,1,0:T(8,128)(2,1)} %fields_hbm.1), custom_call_target="tpu_custom_call" | custom-call | tf_op jit(solution)/shard_map/pallas_call | solution.py:584
  55.2 1.4 %copy.3 = f32[32,256]{1,0:T(8,128)} copy(f32[32,256]{1,0:T(8,128)} %shard_map.17) | data formatting | bytes 65536

commit v6 on v5

--- a/solution.py
+++ b/solution.py
@@ -314,26 +314,30 @@
 
             @pl.when(jnp.logical_and(near >= lo, near < hi))
             def _(width_out=width_out, width_in=width_in):
-                def one(target):
+                def one(target, kind):
                     to_inner = is_inner(target)
 
-                    @pl.when(is_outer(target))
-                    def _():
-                        action(row_copy(lat, target, width_out, False))
-
-                    if width_in:
+                    if kind == 0:
+
+                        @pl.when(is_outer(target))
+                        def _():
+                            action(row_copy(lat, target, width_out, False))
+
+                    if width_in and kind == 1:
 
                         @pl.when(to_inner)
                         def _():
                             action(row_copy(lat, target, width_in, True))
 
-                def both(step, carry):
-                    one(wrapped(lat + (32 - step), LATS))
-                    one(wrapped(lat + (32 + step), LATS))
+                def both(kind, step, carry):
+                    one(wrapped(lat + (32 - step), LATS), kind)
+                    one(wrapped(lat + (32 + step), LATS), kind)
                     return carry
 
-                one(wrapped(lat + 32, LATS))
-                lax.fori_loop(1, 32, both, 0)
+                for kind in (0, 1):
+                    if kind == 0 or width_in:
+                        one(wrapped(lat + 32, LATS), kind)
+                        lax.fori_loop(1, 32, functools.partial(both, kind), 0)
 
     each_row_copy(lambda copy: copy.start())
 

time: 56.7 us -> 56.7 us (level)
  no operation moved by 1% of the time
where the time goes in v6:
time: 56.7 us; the launch traced here: 56.5 us
  Pallas kernels  55.1 us (97%)
  local copies, waits for them, and re-layouts  1.38 us (2%)
    pallas_call x1, Pallas kernels, local(): pl.pallas_call(kernel, out_shape=jax.ShapeDtypeStruct((LOCAL, MONTHS), F3...  55.1 us
    unnamed x1, local copies, waits for them, and re-layouts  1.38 us

profile of v6, /device:TPU:1, one launch (start us, length us, event | category | flops | bytes accessed | tf_op | source)
XLA Modules:
  0.0 56.5 jit_solution(6620912004257569086)
XLA Ops:
  0.0 55.1 %shard_map.17 = f32[32,256]{1,0:T(8,128)} custom-call(bf16[8,32,1024]{2,1,0:T(8,128)(2,1)} %fields_hbm.1), custom_call_target="tpu_custom_call" | custom-call | tf_op jit(solution)/shard_map/pallas_call | solution.py:588
  55.2 1.4 %copy.3 = f32[32,256]{1,0:T(8,128)} copy(f32[32,256]{1,0:T(8,128)} %shard_map.17) | data formatting | bytes 65536

commit v7 on v6

--- a/solution.py
+++ b/solution.py
@@ -262,28 +262,26 @@
     lax.fori_loop(trips_in, trips_out, functools.partial(fill, range(PAIRS_OUT)), pair)
     load.wait()
     flat = fields[...].reshape(BLOCK * LOCAL, NLON)
-    for index in range(PAIRS):
-        first, rows = pair_rows(index)
-        if index < PAIRS_OUT:
-            buffer, place = send_out, index
-        else:
-            buffer, place = send_in, index - PAIRS_OUT
-        spectrum = lax.dot_general(
-            transform[first : first + rows, :],
-            flat,
-            (((1,), (1,)), ((), ())),
-            preferred_element_type=F32,
-        )
-        for odd, part in enumerate(rows_by_latitude(spectrum)):
-            buffer[:, odd, :, place * 128 : (place + 1) * 128] = part.reshape(
-                rows // 8, BLOCK, 128
-            ).astype(BF16)
-
+    def transform_rows(indices):
+        for index in indices:
+            first, rows = pair_rows(index)
+            if index < PAIRS_OUT:
+                buffer, place = send_out, index
+            else:
+                buffer, place = send_in, index - PAIRS_OUT
+            spectrum = lax.dot_general(
+                transform[first : first + rows, :],
+                flat,
+                (((1,), (1,)), ((), ())),
+                preferred_element_type=F32,
+            )
+            for odd, part in enumerate(rows_by_latitude(spectrum)):
+                buffer[:, odd, :, place * 128 : (place + 1) * 128] = part.reshape(
+                    rows // 8, BLOCK, 128
+                ).astype(BF16)
+
+    transform_rows(range(PAIRS_OUT))
     own = jnp.where(inner, lat - MIDDLE, outer_owner(lat))
-
-    @pl.when(inner)
-    def _():
-        got[lat] = send_in[own // 2, own % 2]
 
     @pl.when(outer)
     def _():
@@ -309,7 +307,7 @@
 
     near = jnp.minimum(lat, LATS - 1 - lat)
 
-    def each_row_copy(action):
+    def each_row_copy(action, kinds):
         for lo, hi, width_out, width_in in KINDS:
 
             @pl.when(jnp.logical_and(near >= lo, near < hi))
@@ -334,12 +332,18 @@
                     one(wrapped(lat + (32 + step), LATS), kind)
                     return carry
 
-                for kind in (0, 1):
+                for kind in kinds:
                     if kind == 0 or width_in:
                         one(wrapped(lat + 32, LATS), kind)
                         lax.fori_loop(1, 32, functools.partial(both, kind), 0)
 
-    each_row_copy(lambda copy: copy.start())
+    each_row_copy(lambda copy: copy.start(), (0,))
+    transform_rows(range(PAIRS_OUT, PAIRS))
+    each_row_copy(lambda copy: copy.start(), (1,))
+
+    @pl.when(inner)
+    def _():
+        got[lat] = send_in[own // 2, own % 2]
 
     base = jnp.where(inner, FIRST_IN + own, jnp.where(outer, own, 400))
     stride = jnp.where(inner, INNER, OUTER)
@@ -447,9 +451,14 @@
         for step in steps:
             month_copy(tm, wrapped(tm + step, TMS), part).start()
         share[tm, 0:part, :] = coef[pl.ds(pl.multiple_of(tm * part, part), part), :]
-        for step in steps[::-1]:
-            month_copy(wrapped(tm + step, TMS), tm, part).wait_recv()
-        pieces = [share[source, 0:part, :].astype(F32) for source in range(TMS)]
+        pieces = []
+        for source in range(TMS):
+
+            @pl.when(source != tm)
+            def _(source=source):
+                month_copy(source, tm, part).wait_recv()
+
+            pieces.append(share[source, 0:part, :].astype(F32))
         columns = regroup(pieces).astype(BF16)
         terms = lax.dot_general(
             columns, columns, (((0,), (0,)), ((), ())), preferred_element_type=F32
@@ -498,16 +507,19 @@
         )
 
     def others(away_first, action):
-        order = (2, 1, 3, 0)
-        for away_y in order if away_first else order[::-1]:
+        places = sorted(
+            ((i, j) for i in range(4) for j in range(4)),
+            key=lambda place: sum(min(k, 4 - k) for k in place),
+            reverse=away_first,
+        )
+        for away_y, away_x in places:
             peer_y = wrapped(y + away_y, 4)
-            for away_x in order if away_first else order[::-1]:
-                peer_x = wrapped(x + away_x, 4)
-                for peer_half in (1 - half, half) if away_first else (half, 1 - half):
-                    for peer_core in (1 - core, core):
-                        here = away_y == 0 and away_x == 0
-                        if not (here and peer_half is half and peer_core is core):
-                            action(peer_y, peer_core, peer_x, peer_half)
+            peer_x = wrapped(x + away_x, 4)
+            for peer_half in (1 - half, half) if away_first else (half, 1 - half):
+                for peer_core in (1 - core, core):
+                    here = away_y == 0 and away_x == 0
+                    if not (here and peer_half is half and peer_core is core):
+                        action(peer_y, peer_core, peer_x, peer_half)
 
     others(True, lambda *peer: slab_copy(me, *peer).start())
     slabs[me] = gram[me // 2, me % 2]
@@ -533,7 +545,7 @@
     for away in (4, 3, 5, 2, 6, 1, 7):
         plane_copy(own_pair, wrapped(own_pair + away, 8)).start()
 
-    each_row_copy(lambda copy: copy.wait_send())
+    each_row_copy(lambda copy: copy.wait_send(), (0, 1))
     for applies, part in ((jnp.logical_not(inner), PART_OUT), (inner, PART_IN)):
 
         @pl.when(applies)

time: 56.7 us -> 56.7 us (level)
  no operation moved by 1% of the time
where the time goes in v7:
time: 56.7 us; the launch traced here: 56.5 us
  Pallas kernels  55.1 us (97%)
  local copies, waits for them, and re-layouts  1.38 us (2%)
    pallas_call x1, Pallas kernels, local(): pl.pallas_call(kernel, out_shape=jax.ShapeDtypeStruct((LOCAL, MONTHS), F3...  55.1 us
    unnamed x1, local copies, waits for them, and re-layouts  1.38 us

profile of v7, /device:TPU:1, one launch (start us, length us, event | category | flops | bytes accessed | tf_op | source)
XLA Modules:
  0.0 56.5 jit_solution(3287944534034099351)
XLA Ops:
  0.0 55.1 %shard_map.17 = f32[32,256]{1,0:T(8,128)} custom-call(bf16[8,32,1024]{2,1,0:T(8,128)(2,1)} %fields_hbm.1), custom_call_target="tpu_custom_call" | custom-call | tf_op jit(solution)/shard_map/pallas_call | solution.py:600
  55.1 1.4 %copy.3 = f32[32,256]{1,0:T(8,128)} copy(f32[32,256]{1,0:T(8,128)} %shard_map.17) | data formatting | bytes 65536
